TPU v7x, 256 devices: a whole 4x4x8 slice. The times are simulated.
256 devices in a mesh: row: 16 (over y, x), col: 8 (over z), rep: 2 (over core).
Axes of the slice: x: 4, y: 4, z: 8, core: 2. Of those that a mesh axis runs over, the one named last changes fastest.
Arguments:
- patches: bfloat16 [2, 512, 6144], P('rep', 'col', 'row'), may hold values from -6 to 6
- cotangent: bfloat16 [2, 512, 6144], P('rep', 'col', 'row'), may hold values from -6 to 6
- w_in: bfloat16 [6144, 24576], P('row', 'col'), may hold values from -0.078125 to 0.078125
- w_out: bfloat16 [24576, 6144], P('col', 'row'), may hold values from -0.0390625 to 0.0390625
- moment_in: bfloat16 [2, 6144, 24576], P('rep', 'row', 'col'), may hold values from -2 to 2
- moment_out: bfloat16 [2, 24576, 6144], P('rep', 'col', 'row'), may hold values from -2 to 2
Outputs:
- mixed: bfloat16 [2, 512, 6144], P('rep', 'col', 'row')
- tally_in: bfloat16 [6144, 24576], P('row', 'col')
- tally_out: bfloat16 [24576, 6144], P('col', 'row')
All inputs are finite; a program needn't handle non-finite values.
Results may differ from a plain program's by a relative error of at most 0.0055.
Values may be sent and summed in bfloat16 or wider, within the bound.
A program may use at most 128 MiB of HBM per device.

v0:
```python
import math
import jax
import jax.numpy as jnp
from jax import lax
from jax.sharding import PartitionSpec as P

momentum_decay = 0.9
vote_scale = 0.3


def joined_along(blocks, dim):
    blocks = jnp.moveaxis(blocks, 0, dim)
    lengths = blocks.shape
    return blocks.reshape(*lengths[:dim], lengths[dim] * lengths[dim + 1], *lengths[dim + 2 :])


def sent_to_all(value, axis):
    copies = jnp.broadcast_to(value, (lax.axis_size(axis), *value.shape))
    return lax.all_to_all(copies, axis, split_axis=0, concat_axis=0, tiled=True)


def gather_directly(value, axis, dim):
    return joined_along(sent_to_all(value, axis), dim)


def cut_along(value, dim, peers):
    before, after = (value.shape[:dim], value.shape[dim + 1 :])
    return jnp.moveaxis(value.reshape(*before, peers, -1, *after), dim, 0)


def sum_at_owner(value, axis, dim):
    blocks = cut_along(value, dim, lax.axis_size(axis))
    arrived = lax.all_to_all(blocks, axis, split_axis=0, concat_axis=0, tiled=True)
    return arrived.sum(axis=0)


def gelu_value(pre):
    return 0.5 * pre * (1.0 + lax.erf(pre * (1.0 / math.sqrt(2.0))))


def gelu_slope(pre):
    return 0.5 * (1.0 + lax.erf(pre * (1.0 / math.sqrt(2.0)))) + pre * jnp.exp(-0.5 * pre * pre) * (
        1.0 / math.sqrt(2.0 * math.pi)
    )


def shards(patches, cotangent, w_in, w_out, moment_in, moment_out):
    inputs = gather_directly(patches[0], "col", 0)
    total_rows = inputs.shape[0]
    norm_factor = 1.0 / math.sqrt(total_rows)
    pre_whole = lax.psum(jnp.dot(inputs, w_in, preferred_element_type=jnp.float32), "row")
    hidden = gelu_value(pre_whole).astype(jnp.bfloat16)
    block = hidden
    mixed = sum_at_owner(
        jnp.dot(block, w_out, preferred_element_type=jnp.float32), "col", 0
    ).astype(jnp.bfloat16)
    grads = lax.all_gather(cotangent[0], "col", axis=0, tiled=True)
    block = grads
    back_whole = lax.psum(
        lax.dot_general(
            block, w_out, (((1,), (1,)), ((), ())), preferred_element_type=jnp.float32
        ).astype(jnp.bfloat16),
        "row",
    ).astype(jnp.float32)
    slope = (back_whole * gelu_slope(pre_whole)).astype(jnp.bfloat16)
    grad_first = (
        lax.dot_general(inputs, slope, (((0,), (0,)), ((), ())), preferred_element_type=jnp.float32)
        * norm_factor
    )
    grad_second = (
        lax.dot_general(hidden, grads, (((0,), (0,)), ((), ())), preferred_element_type=jnp.float32)
        * norm_factor
    )
    moved_first = (
        momentum_decay * moment_in[0].astype(jnp.float32) + (1.0 - momentum_decay) * grad_first
    )
    moved_second = (
        momentum_decay * moment_out[0].astype(jnp.float32) + (1.0 - momentum_decay) * grad_second
    )
    vote_first = jnp.tanh(moved_first / vote_scale).astype(jnp.bfloat16)
    vote_second = jnp.tanh(moved_second / vote_scale).astype(jnp.bfloat16)
    tally_first, tally_second = (
        lax.psum(vote_first, "rep").astype(jnp.float32),
        lax.psum(vote_second, "rep").astype(jnp.float32),
    )
    return (mixed[None], tally_first.astype(jnp.bfloat16), tally_second.astype(jnp.bfloat16))


def solution(mesh):
    in_specs = (
        P("rep", "col", "row"),
        P("rep", "col", "row"),
        P("row", "col"),
        P("col", "row"),
        P("rep", "row", "col"),
        P("rep", "col", "row"),
    )
    out_specs = (P("rep", "col", "row"), P("row", "col"), P("col", "row"))
    return jax.shard_map(shards, mesh=mesh, in_specs=in_specs, out_specs=out_specs, check_vma=False)
```

profile of v0, /device:TPU:1, one launch (start us, length us, event | category | flops | bytes accessed | tf_op | source)
XLA Modules:
  0.0 338.2 jit_solution(2649844550422343762)
XLA Ops:
  7.2 0.0 copy-start
  7.2 0.0 all-reduce.5.cloned.1.call-start
  7.2 1.0 broadcast_in_dim.4
  8.2 22.4 %all_to_all.10 = bf16[8,64,384]{2,1,0:T(8,128)(2,1)S(1)} all-to-all(bf16[8,64,384]{2,1,0:T(8,128)(2,1)S(1)} %broadcast_in_dim.4), channel_id=1, replica_groups=mesh['row'=16,'col'=8,'rep'=2] {'col'}, dimensions={0} | all-to-all | bytes 786432 | tf_op jit(solution)/shard_map/all_to_all | solution.py:19
  30.6 6.1 %fusion.20 = f32[512,3072]{1,0:T(8,128)} fusion(bf16[512,384]{1,0:T(8,128)(2,1)S(1)} %bitcast.36, bf16[384,3072]{1,0:T(8,128)(2,1)} %param.8), kind=kOutput, calls=%fused_computation.26 | convolution fusion | flops 1207959552 | bytes 9043968 | tf_op jit(solution)/shard_map/dot_general | solution.py:51
  36.7 0.0 copy-start.2
  36.7 0.0 all-reduce.5.cloned.1.call-update
  36.7 0.0 all-reduce.7.cloned.1.call-start
  36.8 0.7 copy-done.2
  37.5 20.5 %all-gather = bf16[1,512,384]{2,1,0:T(8,128)(2,1)S(1)} all-gather(bf16[1,64,384]{2,1,0:T(8,128)(2,1)S(1)} %copy-done.2), channel_id=2, replica_groups=mesh['row'=16,'col'=8,'rep'=2] {'col'}, dimensions={1}, use_global_device_ids=true | all-gather | bytes 442368 | tf_op jit(solution)/shard_map/all_gather | solution.py:57
  58.0 0.0 copy-done
  58.0 3.5 %convolution_convert_fusion = bf16[512,3072]{1,0:T(8,128)(2,1)} fusion(bf16[3072,384]{1,0:T(8,128)(2,1)S(1)} %copy-done, bf16[1,512,384]{2,1,0:T(8,128)(2,1)S(1)} %all-gather), kind=kOutput, calls=%fused_computation.17 | convolution fusion | flops 1209532416 | bytes 5898240 | tf_op jit(solution)/shard_map/dot_general | solution.py:60
  61.4 0.0 all-reduce.7.cloned.1.call-update
  61.5 0.0 all-reduce.9.cloned.1.call-start
  61.5 4.3 %copy.9 = bf16[1,384,3072]{1,2,0:T(8,128)(2,1)} copy(bf16[1,384,3072]{2,1,0:T(8,128)(2,1)} %param.10) | data formatting | bytes 4718592 | tf_op args[4]
  65.8 101.0 %all-reduce.5.cloned.1.call-done = f32[512,3072]{1,0:T(8,128)} async-done(((f32[512,3072]{1,0:T(8,128)}), f32[512,3072]{1,0:T(8,128)}) %all-reduce.5.cloned.1.call-update) | async-done | bytes 6291472 | tf_op jit(solution)/shard_map/psum | solution.py:51
  166.8 0.0 copy-start.3
  166.8 3.6 %multiply_convert_fusion = bf16[512,3072]{1,0:T(8,128)(2,1)S(1)} fusion(f32[512,3072]{1,0:T(8,128)} %all-reduce.5.cloned.1.call-done), kind=kLoop, calls=%fused_computation.7 | loop fusion | flops 7864320 | bytes 9437184 | tf_op jit(solution)/shard_map/convert_element_type | solution.py:52
  170.4 0.0 copy-start.1
  170.4 1.7 copy-done.1
  172.1 0.0 copy-done.3
  172.1 4.0 %fusion.8 = bf16[3072,384]{1,0:T(8,128)(2,1)} fusion(bf16[1,3072,384]{2,1,0:T(8,128)(2,1)S(1)} %copy-done.3, bf16[512,3072]{1,0:T(8,128)(2,1)S(1)} %multiply_convert_fusion, bf16[1,512,384]{2,1,0:T(8,128)(2,1)S(1)} %all-gather), kind=kOutput, calls=%fused_computation.12 | convolution fusion | flops 1215037440 | bytes 8257536 | tf_op jit(solution)/shard_map/dot_general | solution.py:71
  176.1 99.6 %all-reduce.7.cloned.1.call-done = bf16[512,3072]{1,0:T(8,128)(2,1)} async-done(((bf16[512,3072]{1,0:T(8,128)(2,1)}), bf16[512,3072]{1,0:T(8,128)(2,1)}) %all-reduce.7.cloned.1.call-update) | async-done | bytes 3145744 | tf_op jit(solution)/shard_map/psum | solution.py:59
  275.7 8.4 %fusion.11 = bf16[384,3072]{0,1:T(8,128)(2,1)} fusion(bf16[1,384,3072]{1,2,0:T(8,128)(2,1)} %copy.9, bf16[512,384]{1,0:T(8,128)(2,1)S(1)} %bitcast.37, f32[512,3072]{1,0:T(8,128)} %all-reduce.5.cloned.1.call-done, bf16[512,3072]{1,0:T(8,128)(2,1)} %all-reduce.7.cloned.1.call-done), kind=kOutput, calls=%fused_computation.16 | convolution fusion | flops 1232338944 | bytes 14548992 | tf_op jit(solution)/shard_map/dot_general | solution.py:67
  284.1 0.0 all-reduce.9.cloned.1.call-update
  284.1 3.7 %fusion.21 = f32[512,384]{1,0:T(8,128)S(1)} fusion(bf16[512,3072]{1,0:T(8,128)(2,1)} %copy-done.1, bf16[3072,384]{1,0:T(8,128)(2,1)S(1)} %copy-done), kind=kOutput, calls=%fused_computation.27 | convolution fusion | flops 1207959552 | bytes 6291456 | tf_op jit(solution)/shard_map/dot_general | solution.py:55
  287.8 27.9 %all_to_all.11 = f32[8,64,384]{2,1,0:T(8,128)S(1)} all-to-all(f32[8,64,384]{2,1,0:T(8,128)S(1)} %bitcast.38), channel_id=1, replica_groups=mesh['row'=16,'col'=8,'rep'=2] {'col'}, dimensions={0} | all-to-all | bytes 1572864 | tf_op jit(solution)/shard_map/all_to_all | solution.py:33
  315.7 0.7 reduce_sum.9
  316.4 7.7 %all-reduce.9.cloned.1.call-done = (bf16[384,3072]{0,1:T(8,128)(2,1)}, bf16[3072,384]{1,0:T(8,128)(2,1)}) async-done(((bf16[384,3072]{0,1:T(8,128)(2,1)}, bf16[3072,384]{1,0:T(8,128)(2,1)}), (bf16[384,3072]{0,1:T(8,128)(2,1)}, bf16[3072,384]{1,0:T(8,128)(2,1)})) %all-reduce.9.cloned.1.call-update) | async-done | bytes 4718608 | tf_op jit(solution)/shard_map/psum | solution.py:83
  324.1 4.3 %copy.10 = bf16[384,3072]{1,0:T(8,128)(2,1)} copy(bf16[384,3072]{0,1:T(8,128)(2,1)} %get-tuple-element.6) | data formatting | bytes 4718592
  328.4 3.3 copy.15
Async XLA Ops:
  7.2 50.8 %copy-start = (bf16[3072,384]{1,0:T(8,128)(2,1)S(1)}, bf16[3072,384]{1,0:T(8,128)(2,1)}, u32[]{:S(2)}) copy-start(bf16[3072,384]{1,0:T(8,128)(2,1)} %param.9) | copy-start | bytes 7077892
  7.2 159.7 %all-reduce.5.cloned.1.call-start = ((), (), s32[]{:S(2)}) async-start(), calls=%async_computation.2 | async-start | bytes 12582912 | tf_op jit(solution)/shard_map/psum | solution.py:51
  36.7 0.8 copy-start.2
  36.7 239.0 %all-reduce.7.cloned.1.call-start = ((), (), s32[]{:S(2)}) async-start(), calls=%async_computation.3 | async-start | bytes 6291456 | tf_op jit(solution)/shard_map/psum | solution.py:59
  61.5 262.7 %all-reduce.9.cloned.1.call-start = ((), (), s32[]{:S(2)}) async-start(), calls=%async_computation.4 | async-start | bytes 9437184 | tf_op jit(solution)/shard_map/psum | solution.py:83
  166.8 5.3 %copy-start.3 = (bf16[1,3072,384]{2,1,0:T(8,128)(2,1)S(1)}, bf16[1,3072,384]{2,1,0:T(8,128)(2,1)}, u32[]{:S(2)}) copy-start(bf16[1,3072,384]{2,1,0:T(8,128)(2,1)} %param.11) | copy-start | bytes 7077892
  170.4 1.7 copy-start.1
Sparse Core Ops, SparseCore 0:
  36.9 129.9 all-reduce.4
  170.2 105.4 all-reduce.6
  284.2 39.8 all-reduce.8
where the time goes:
time: 339 us; the launch traced here: 338 us
  waiting for transfers between devices  208 us (61%)
  blocking collectives  70.8 us (21%)
  matrix products  25.6 us (8%)
  local copies, waits for them, and re-layouts  15.3 us (5%)
  between operations  13.8 us (4%)
  other arithmetic  4.23 us (1%)
    psum x1, waiting for transfers between devices, shards(): lax.psum(jnp.dot(inputs, w_in, preferred_element_type=jnp.float32), 'row')  101 us
    psum x1, waiting for transfers between devices, shards(): lax.psum(lax.dot_general(block, w_out, (((1,), (1,)), ((), ())), preferre...  99.6 us
    all_to_all x1, blocking collectives, sum_at_owner(): lax.all_to_all(blocks, axis, split_axis=0, concat_axis=0, tiled=True)  27.9 us
    all_to_all x1, blocking collectives, sent_to_all(): return lax.all_to_all(copies, axis, split_axis=0, concat_axis=0, tiled=True)  22.4 us
    all_gather x1, blocking collectives, shards(): grads = lax.all_gather(cotangent[0], 'col', axis=0, tiled=True)  20.5 us
    unnamed x11, local copies, waits for them, and re-layouts  14.3 us
    dot_general x1, matrix products, shards(): lax.dot_general(inputs, slope, (((0,), (0,)), ((), ())), preferred_elemen...  8.39 us
    psum x1, waiting for transfers between devices, shards(): lax.psum(vote_first, 'rep').astype(jnp.float32)  7.74 us
  transfers between devices with their start and end apart: 3, of which 3 were waited for; matrix products, arithmetic and copies ran while one was open for 6% of the time, Pallas kernels for 0%

commit v1 on v0

--- a/solution.py
+++ b/solution.py
@@ -6,6 +6,11 @@
 
 momentum_decay = 0.9
 vote_scale = 0.3
+
+
+def add_all(shard, axis):
+    terms = lax.all_gather(shard, axis)
+    return jnp.sum(terms, axis=0)
 
 
 def joined_along(blocks, dim):
@@ -56,7 +61,7 @@
     ).astype(jnp.bfloat16)
     grads = lax.all_gather(cotangent[0], "col", axis=0, tiled=True)
     block = grads
-    back_whole = lax.psum(
+    back_whole = add_all(
         lax.dot_general(
             block, w_out, (((1,), (1,)), ((), ())), preferred_element_type=jnp.float32
         ).astype(jnp.bfloat16),

time: 339 us -> 539 us (1.59)
  waiting for transfers between devices: 208 us -> 390 us
  other arithmetic: 4.23 us -> 22.8 us
    all_gather x0 -> x1, waiting for transfers between devices: none -> 281 us  [add_all(): terms = lax.all_gather(shard, axis)]
    psum x1 -> x0, waiting for transfers between devices: 99.6 us -> none  [shards(): lax.psum(lax.dot_general(block, w_out, (((1,), (1,)), ((), ())), preferre...]
    reduce_sum x0 -> x1, other arithmetic: none -> 18.6 us  [add_all(): return jnp.sum(terms, axis=0)]
  transfers between devices with their start and end apart: 3 -> 3, of which waited for: 3 -> 3; matrix products, arithmetic and copies ran while one was open for 6% -> 4% of each run, Pallas kernels for 0% -> 0%
where the time goes in v1:
time: 539 us; the launch traced here: 538 us
  waiting for transfers between devices  390 us (72%)
  blocking collectives  70.9 us (13%)
  matrix products  25.6 us (5%)
  other arithmetic  22.8 us (4%)
  local copies, waits for them, and re-layouts  15.3 us (3%)
  between operations  13.8 us (3%)
    all_gather x1, waiting for transfers between devices, add_all(): terms = lax.all_gather(shard, axis)  281 us
    psum x1, waiting for transfers between devices, shards(): lax.psum(jnp.dot(inputs, w_in, preferred_element_type=jnp.float32), 'row')  101 us
    all_to_all x1, blocking collectives, sum_at_owner(): lax.all_to_all(blocks, axis, split_axis=0, concat_axis=0, tiled=True)  28 us
    all_to_all x1, blocking collectives, sent_to_all(): return lax.all_to_all(copies, axis, split_axis=0, concat_axis=0, tiled=True)  22.4 us
    all_gather x1, blocking collectives, shards(): grads = lax.all_gather(cotangent[0], 'col', axis=0, tiled=True)  20.5 us
    reduce_sum x1, other arithmetic, add_all(): return jnp.sum(terms, axis=0)  18.6 us
    unnamed x11, local copies, waits for them, and re-layouts  14.3 us
  transfers between devices with their start and end apart: 3, of which 3 were waited for; matrix products, arithmetic and copies ran while one was open for 4% of the time, Pallas kernels for 0%

profile of v1, /device:TPU:1, one launch (start us, length us, event | category | flops | bytes accessed | tf_op | source)
XLA Modules:
  0.0 538.5 jit_solution(16435453833850260729)
XLA Ops:
  7.2 0.0 copy-start
  7.2 0.0 all-reduce.4.cloned.1.call-start
  7.2 1.0 broadcast_in_dim.4
  8.2 22.4 %all_to_all.10 = bf16[8,64,384]{2,1,0:T(8,128)(2,1)S(1)} all-to-all(bf16[8,64,384]{2,1,0:T(8,128)(2,1)S(1)} %broadcast_in_dim.4), channel_id=1, replica_groups=mesh['row'=16,'col'=8,'rep'=2] {'col'}, dimensions={0} | all-to-all | bytes 786432 | tf_op jit(solution)/shard_map/all_to_all | solution.py:24
  30.6 6.1 %fusion.20 = f32[512,3072]{1,0:T(8,128)} fusion(bf16[512,384]{1,0:T(8,128)(2,1)S(1)} %bitcast.38, bf16[384,3072]{1,0:T(8,128)(2,1)} %param.8), kind=kOutput, calls=%fused_computation.26 | convolution fusion | flops 1207959552 | bytes 9043968 | tf_op jit(solution)/shard_map/dot_general | solution.py:56
  36.7 0.0 copy-start.2
  36.7 0.0 all-reduce.4.cloned.1.call-update
  36.7 0.0 all-gather.4.cloned.1.call-start
  36.7 0.7 copy-done.2
  37.5 20.5 %all-gather = bf16[1,512,384]{2,1,0:T(8,128)(2,1)S(1)} all-gather(bf16[1,64,384]{2,1,0:T(8,128)(2,1)S(1)} %copy-done.2), channel_id=2, replica_groups=mesh['row'=16,'col'=8,'rep'=2] {'col'}, dimensions={1}, use_global_device_ids=true | all-gather | bytes 442368 | tf_op jit(solution)/shard_map/all_gather | solution.py:62
  57.9 0.0 copy-done
  57.9 3.5 convolution_convert_fusion
  61.4 0.0 all-gather.4.cloned.1.call-update
  61.4 0.0 all-reduce.6.cloned.1.call-start
  61.5 4.3 copy.9
  65.8 101.0 %all-reduce.4.cloned.1.call-done = f32[512,3072]{1,0:T(8,128)} async-done(((f32[512,3072]{1,0:T(8,128)}), f32[512,3072]{1,0:T(8,128)}) %all-reduce.4.cloned.1.call-update) | async-done | bytes 6291472 | tf_op jit(solution)/shard_map/psum | solution.py:56
  166.8 0.0 copy-start.3
  166.8 3.6 multiply_convert_fusion
  170.4 0.0 copy-start.1
  170.4 1.7 copy-done.1
  172.0 0.0 copy-done.3
  172.0 4.0 fusion.8
  176.0 280.8 %all-gather.4.cloned.1.call-done = bf16[8192,3072]{1,0:T(8,128)(2,1)} async-done(((bf16[512,3072]{1,0:T(8,128)(2,1)}), bf16[8192,3072]{1,0:T(8,128)(2,1)}) %all-gather.4.cloned.1.call-update) | async-done | bytes 50331664 | tf_op jit(solution)/shard_map/all_gather | solution.py:12
  456.8 18.6 %reduce_sum.22 = bf16[512,3072]{1,0:T(8,128)(2,1)} reduce(bf16[16,512,3072]{2,1,0:T(8,128)(2,1)} %bitcast.37, bf16[]{:T(256)} %constant.6.clone.1), dimensions={0}, to_apply=%region_2.0 | reduce | flops 23592960 | bytes 53477376 | tf_op jit(solution)/shard_map/reduce_sum | solution.py:13
  475.4 8.4 %fusion.11 = bf16[384,3072]{0,1:T(8,128)(2,1)} fusion(bf16[1,384,3072]{1,2,0:T(8,128)(2,1)} %copy.9, bf16[512,384]{1,0:T(8,128)(2,1)S(1)} %bitcast.39, f32[512,3072]{1,0:T(8,128)} %all-reduce.4.cloned.1.call-done, bf16[512,3072]{1,0:T(8,128)(2,1)} %reduce_sum.22), kind=kOutput, calls=%fused_computation.16 | convolution fusion | flops 1232338944 | bytes 14548992 | tf_op jit(solution)/shard_map/dot_general | solution.py:72
  483.8 0.0 all-reduce.6.cloned.1.call-update
  483.8 3.7 fusion.21
  487.5 28.0 %all_to_all.11 = f32[8,64,384]{2,1,0:T(8,128)S(1)} all-to-all(f32[8,64,384]{2,1,0:T(8,128)S(1)} %bitcast.40), channel_id=1, replica_groups=mesh['row'=16,'col'=8,'rep'=2] {'col'}, dimensions={0} | all-to-all | bytes 1572864 | tf_op jit(solution)/shard_map/all_to_all | solution.py:38
  515.6 0.7 reduce_sum.21
  516.2 8.1 %all-reduce.6.cloned.1.call-done = (bf16[384,3072]{0,1:T(8,128)(2,1)}, bf16[3072,384]{1,0:T(8,128)(2,1)}) async-done(((bf16[384,3072]{0,1:T(8,128)(2,1)}, bf16[3072,384]{1,0:T(8,128)(2,1)}), (bf16[384,3072]{0,1:T(8,128)(2,1)}, bf16[3072,384]{1,0:T(8,128)(2,1)})) %all-reduce.6.cloned.1.call-update) | async-done | bytes 4718608 | tf_op jit(solution)/shard_map/psum | solution.py:88
  524.4 4.3 copy.10
  528.6 3.3 copy.14
Async XLA Ops:
  7.2 50.8 %copy-start = (bf16[3072,384]{1,0:T(8,128)(2,1)S(1)}, bf16[3072,384]{1,0:T(8,128)(2,1)}, u32[]{:S(2)}) copy-start(bf16[3072,384]{1,0:T(8,128)(2,1)} %param.9) | copy-start | bytes 7077892
  7.2 159.6 %all-reduce.4.cloned.1.call-start = ((), (), s32[]{:S(2)}) async-start(), calls=%async_computation.2 | async-start | bytes 12582912 | tf_op jit(solution)/shard_map/psum | solution.py:56
  36.7 0.8 copy-start.2
  36.7 420.2 %all-gather.4.cloned.1.call-start = ((), (), s32[]{:S(2)}) async-start(), calls=%async_computation.3 | async-start | bytes 53477376 | tf_op jit(solution)/shard_map/all_gather | solution.py:12
  61.4 462.9 %all-reduce.6.cloned.1.call-start = ((), (), s32[]{:S(2)}) async-start(), calls=%async_computation.4 | async-start | bytes 9437184 | tf_op jit(solution)/shard_map/psum | solution.py:88
  166.8 5.3 copy-start.3
  170.4 1.7 copy-start.1
Sparse Core Ops, SparseCore 0:
  36.8 129.9 all-reduce.3
  169.2 287.5 all-gather.3
  484.0 40.3 all-reduce.5
